TPU v7x, 256 devices: a whole 4x4x8 slice. The times are simulated.
256 devices in a mesh: rows: 64 (over x, z, y_hi), cols: 4 (over y_lo, core).
Axes of the slice: x: 4, y: 4 (y_hi: 2, y_lo: 2; y = y_hi * 2 + y_lo), z: 8, core: 2. Of those that a mesh axis runs over, the one named last changes fastest.
Arguments:
- matrix: float32 [4096, 32, 2, 128], P('rows', 'cols'), may hold values from -54 to 54
- plan: int32 [2, 4, 256], replicated, may hold values from 0 to 255, as said below
Outputs:
- rotated: float32 [4096, 32, 2, 128], P('rows', 'cols')
Inputs may be any that keep to these rules, and one draw needn't show every extreme that they name: Each plan[s, r] pairs the 256 columns: partner of partner of i is i, and no column is its own partner.
All inputs are finite; a program needn't handle non-finite values.
Results may differ from a plain program's by a relative error of at most 0.0003.
Values sent between devices are 32-bit elements; how exact they have to be, the bound alone decides.
A program may use at most 128 MiB of HBM per device.

v0:
```python
import functools

import jax
import jax.numpy as jnp
from jax import lax
from jax.experimental import pallas as pl
from jax.experimental.pallas import tpu as pltpu
from jax.sharding import PartitionSpec as P

MESH = pl.DeviceIdType.MESH
XS, ZS, YS, CS = 4, 8, 2, 4
GROUP = XS * YS
BLOCK = 128
WIDTH = 2 * BLOCK
PEERS = ((2, 1), (0, 1), (1, 1), (2, 0), (3, 1), (1, 0), (3, 0))
RING = (4, 3, 5, 2, 6, 1, 7)
FIRST = (((0,), (0,)), ((), ()))
PLAIN = (((1,), (0,)), ((), ()))


def parts_of(value):
    high = value.astype(jnp.bfloat16)
    rest = value - high.astype(jnp.float32)
    middle = rest.astype(jnp.bfloat16)
    low = (rest - middle.astype(jnp.float32)).astype(jnp.bfloat16)
    return high, middle, low


def product(a, b, dims):
    return lax.dot_general(a, b, dims, preferred_element_type=jnp.float32)


def full_product(a, b, dims=PLAIN):
    return lax.dot_general(
        a, b, dims, precision=lax.Precision.HIGHEST, preferred_element_type=jnp.float32
    )


def product_of(a, b, dims=PLAIN):
    high = product(a[0], b[0], dims)
    return high + (product(a[0], b[1], dims) + product(a[1], b[0], dims))


def times_onehot(value, partner):
    rows = lax.broadcasted_iota(jnp.int32, (WIDTH, WIDTH), 0)
    onehot = (rows == partner).astype(jnp.float32).astype(jnp.bfloat16)
    high, middle, low = parts_of(value)
    return product(high, onehot, PLAIN) + (product(middle, onehot, PLAIN) + product(low, onehot, PLAIN))


def turned_by(rotation, partner, cosine, sine):
    if rotation is None:
        below = lax.broadcasted_iota(jnp.int32, (WIDTH, WIDTH), 0)
        along = lax.broadcasted_iota(jnp.int32, (WIDTH, WIDTH), 1)
        return jnp.where(below == along, cosine, 0.0) + jnp.where(below == partner, sine, 0.0)
    return rotation * cosine + times_onehot(rotation, partner) * sine


def columns_moved(value, partner):
    rows = value.shape[0]
    near = jnp.where(partner < BLOCK, partner, partner - BLOCK)
    sides = []
    for half in range(2):
        lanes = slice(half * BLOCK, (half + 1) * BLOCK)
        index = jnp.broadcast_to(near[:, lanes], (rows, BLOCK))
        left = jnp.broadcast_to(partner[:, lanes] < BLOCK, (rows, BLOCK))
        picked = [
            jnp.take_along_axis(value[:, n * BLOCK : (n + 1) * BLOCK], index, axis=1, mode="promise_in_bounds")
            for n in range(2)
        ]
        sides.append(jnp.where(left, picked[0], picked[1]))
    return jnp.concatenate(sides, axis=1)


def solve(gram, plan_of_round, rounds, tell):
    below = lax.broadcasted_iota(jnp.int32, (WIDTH, WIDTH), 0)
    along = lax.broadcasted_iota(jnp.int32, (WIDTH, WIDTH), 1)
    index = lax.broadcasted_iota(jnp.int32, (1, WIDTH), 1)
    rotation = None
    image = gram
    for r in range(rounds):
        partner = plan_of_round(r)
        if r == 0:
            unit = below == along
            pairing = below == partner
            own = jnp.sum(jnp.where(unit, gram, 0.0), axis=0, keepdims=True)
            cross = jnp.sum(jnp.where(pairing, gram, 0.0), axis=0, keepdims=True)
        else:
            own = jnp.sum(rotation * image, axis=0, keepdims=True)
            rotation_moved = columns_moved(rotation, partner)
            cross = jnp.sum(rotation_moved * image, axis=0, keepdims=True)
        other = columns_moved(jnp.broadcast_to(own, (8, WIDTH)), partner)[:1]
        orient = jnp.where(index < partner, 1.0, -1.0)
        spread = orient * (other - own)
        sign = jnp.where(spread >= 0.0, 1.0, -1.0)
        tangent = sign * 2.0 * cross / (jnp.abs(spread) + jnp.sqrt(spread * spread + 4.0 * cross * cross))
        cosine = lax.rsqrt(1.0 + tangent * tangent)
        sine = -orient * (tangent * cosine)
        tell(r, cosine, sine)
        if r == 0:
            rotation = jnp.where(unit, cosine, 0.0) + jnp.where(pairing, sine, 0.0)
        else:
            rotation = rotation * cosine + rotation_moved * sine
        image = image * cosine + columns_moved(image, partner) * sine
    return rotation, image


def kernel(
    x_hbm,
    plan_hbm,
    result,
    plan_ref,
    x_own,
    tops,
    bottoms,
    partial,
    shares_tt,
    shares_b,
    total,
    total_mine,
    next_tops,
    next_bottoms,
    turns_out,
    turns_in,
    bottoms_in,
    square_out,
    square_in,
    tops_now,
    between,
    shares_c,
    half_turned,
    half_turned_mine,
    result_out,
    load_sem,
    in_send,
    in_recv,
    sum_send,
    sum_recv,
    all_send,
    all_recv,
    next_send,
    next_recv,
    cross_send,
    cross_recv,
    all2_send,
    all2_recv,
    out_send,
    out_recv,
):
    rows = lax.axis_index("rows")
    col = lax.axis_index("cols")
    x = rows // (ZS * YS)
    z = (rows // YS) % ZS
    y = rows % YS
    me = x * YS + y
    chunk = x_own.shape[1]
    every = tops.shape[0]
    share = BLOCK // ZS
    near, ring = len(PEERS), len(RING)
    early = near // 2

    def member(a, b):
        return ((x + a) % XS) * YS + (y + b) % YS

    def row_of(a, b):
        return (((x + a) % XS) * ZS + z) * YS + (y + b) % YS

    def ring_row(d):
        return (x * ZS + (z + d) % ZS) * YS + y

    after = (col + 1) % CS
    before = (col + CS - 1) % CS

    def send(src, dst, send_sem, recv_sem, row, column):
        pltpu.make_async_remote_copy(
            src_ref=src, dst_ref=dst, send_sem=send_sem, recv_sem=recv_sem, device_id=(row, column), device_id_type=MESH
        ).start()

    def await_bytes(like, sem):
        pltpu.make_async_remote_copy(
            src_ref=like, dst_ref=like, send_sem=sem, recv_sem=sem, device_id=(rows, col), device_id_type=MESH
        ).wait_recv()

    barrier = pltpu.get_barrier_semaphore()

    def greet(row, column):
        pl.semaphore_signal(barrier, inc=1, device_id=(row, column), device_id_type=MESH)

    for a, b in PEERS:
        greet(row_of(a, b), col)
        greet(row_of(a, b), before)
    greet(rows, before)
    for d in RING:
        greet(ring_row(d), col)

    own_place = pl.ds(pl.multiple_of(me * chunk, chunk), chunk)
    loads = ([], [])
    for half in range(2):
        for a, b in PEERS:
            slot = 2 * member(a, b) + half
            loads[half].append(pltpu.make_async_copy(x_hbm.at[:, slot, :], x_own.at[slot], load_sem.at[half]))
        gathered = (tops, bottoms)[half]
        loads[half].append(pltpu.make_async_copy(x_hbm.at[:, 2 * me + half, :], gathered.at[own_place], load_sem.at[half]))
        for load in loads[half]:
            load.start()
    plan_copy = pltpu.make_async_copy(plan_hbm, plan_ref, load_sem.at[2])
    plan_copy.start()

    pl.delay(1)
    pl.semaphore_wait(barrier, 2 * near + 1 + ring)

    pl.delay(1)
    for half in range(2):
        gathered = (tops, bottoms)[half]
        for load in loads[half]:
            load.wait()
        for k, (a, b) in enumerate(PEERS):
            send(
                x_own.at[2 * member(a, b) + half],
                gathered.at[own_place],
                in_send,
                in_recv.at[half, int(k >= early)],
                row_of(a, b),
                col,
            )
    plan_copy.wait()

    def ring_place(d):
        return pl.ds(pl.multiple_of(((z + d) % ZS) * share, share), share)

    pl.delay(1)
    def lines_of(gathered, batch):
        offsets = ((0, 0), *PEERS[:early]) if batch == 0 else PEERS[early:]
        places = [pl.ds(pl.multiple_of(member(XS - a, YS - b) * chunk, chunk), chunk) for a, b in offsets]
        return jnp.concatenate([gathered[place] for place in places], axis=0)

    def arrived(gathered, half, batch):
        count = near - early if batch else early
        await_bytes(gathered.at[: count * chunk], in_recv.at[half, batch])

    arrived(tops, 0, 0)
    tops_early = lines_of(tops, 0)
    square_early = full_product(tops_early, tops_early, FIRST)
    arrived(tops, 0, 1)
    pl.delay(1)
    @pl.when(col % 2 == 0)
    def _():
        send(tops, next_tops, next_send, next_recv.at[0], rows, after)

    tops_late = lines_of(tops, 1)
    partial[0] = square_early + full_product(tops_late, tops_late, FIRST)
    for n, d in enumerate(RING):
        send(partial.at[0, ring_place(d)], shares_tt.at[n], sum_send, sum_recv.at[0], ring_row(d), col)

    pl.delay(1)
    arrived(bottoms, 1, 0)
    bottoms_early = lines_of(bottoms, 0)
    both_early = full_product(bottoms_early, jnp.concatenate([tops_early, bottoms_early], axis=1), FIRST)
    arrived(bottoms, 1, 1)
    pl.delay(1)
    bottoms_late = lines_of(bottoms, 1)
    both = both_early + full_product(bottoms_late, jnp.concatenate([tops_late, bottoms_late], axis=1), FIRST)
    partial[1] = both[:, :BLOCK]
    partial[2] = both[:, BLOCK:]
    for n, d in enumerate(RING):
        send(partial.at[1:3, ring_place(d)], shares_b.at[n], sum_send, sum_recv.at[1], ring_row(d), col)

    @pl.when(col % 2 == 1)
    def _():
        send(tops, next_tops, next_send, next_recv.at[0], rows, after)

    send(bottoms, next_bottoms, next_send, next_recv.at[1], rows, after)

    def cross_products(half):
        arrived_block = (next_tops, next_bottoms)[half]
        await_bytes(arrived_block, next_recv.at[half])
        columns = parts_of(jnp.concatenate([tops[...], bottoms[...]], axis=1))
        between[half] = product_of(parts_of(arrived_block[...]), columns, FIRST)
        for n, d in enumerate(RING):
            send(between.at[half, ring_place(d)], shares_c.at[half, n], cross_send, cross_recv.at[half], ring_row(d), col)

    pl.delay(1)
    cross_products(0)

    pl.delay(1)
    here = ring_place(0)
    await_bytes(shares_tt, sum_recv.at[0])
    mine = partial[0, here]
    for n in range(ring):
        mine = mine + shares_tt[n]
    total_mine[0] = mine
    total[0, here] = mine
    for d in RING:
        send(total_mine.at[0], total.at[0, here], all_send, all_recv.at[0], ring_row(d), col)
    await_bytes(shares_b, sum_recv.at[1])
    mine = partial[1:3, here]
    for n in range(ring):
        mine = mine + shares_b[n]
    total_mine[1:3] = mine
    total[1:3, here] = mine
    for d in RING:
        send(total_mine.at[1:3], total.at[1:3, here], all_send, all_recv.at[1], ring_row(d), col)
    pl.delay(1)
    cross_products(1)
    pl.delay(1)
    await_bytes(total.at[0, : ring * share], all_recv.at[0])
    await_bytes(total.at[1:3, : ring * share], all_recv.at[1])

    pl.delay(1)
    cross = total[1]
    gram = jnp.concatenate(
        [jnp.concatenate([total[0], jnp.transpose(cross)], axis=1), jnp.concatenate([cross, total[2]], axis=1)], axis=0
    )
    rounds = plan_ref.shape[1]

    def first_plan(r):
        return plan_ref[0, r : r + 1, :]

    def tell(r, cosine, sine):
        turns_out[r] = jnp.concatenate([cosine, sine], axis=0)
        send(turns_out.at[r], turns_in.at[r], next_send, next_recv.at[2 + r], rows, after)

    rotation, image = solve(gram, first_plan, rounds, tell)
    pl.delay(1)
    await_bytes(shares_c.at[0], cross_recv.at[0])
    await_bytes(shares_c.at[1], cross_recv.at[1])
    pl.delay(1)
    mine = between[:, here]
    for n in range(ring):
        mine = mine + shares_c[:, n]
    turn = parts_of(rotation)
    left = [part[:, :BLOCK] for part in turn]
    mine = product_of(parts_of(mine.reshape(2 * share, WIDTH)), left).reshape(2, share, BLOCK)
    half_turned_mine[...] = mine
    half_turned[:, here] = mine
    for d in RING:
        send(half_turned_mine, half_turned.at[:, here], all2_send, all2_recv, ring_row(d), col)
    pl.delay(1)
    square_out[...] = full_product(rotation[:, BLOCK:], image[:, BLOCK:], FIRST)
    top_square = full_product(rotation[:, :BLOCK], image[:, :BLOCK], FIRST)
    send(square_out, square_in, next_send, next_recv.at[2 + rounds], rows, after)

    pl.delay(1)
    columns = parts_of(jnp.concatenate([tops[...], bottoms[...]], axis=1))
    tops_now[...] = product_of(columns, left)
    next_rotation = None
    for r in range(rounds):
        await_bytes(turns_in.at[r], next_recv.at[2 + r])
        next_rotation = turned_by(next_rotation, first_plan(r), turns_in[r, 0:1, :], turns_in[r, 1:2, :])
    right = [part[:, BLOCK:] for part in parts_of(next_rotation)]
    next_columns = parts_of(jnp.concatenate([next_tops[...], next_bottoms[...]], axis=1))
    bottoms_in[...] = product_of(next_columns, right)
    pl.delay(1)
    await_bytes(square_in, next_recv.at[2 + rounds])
    await_bytes(half_turned.at[:, : ring * share], all2_recv)
    pl.delay(1)
    cross = product_of(parts_of(half_turned[...].reshape(WIDTH, BLOCK)), right, FIRST)
    gram = jnp.concatenate(
        [jnp.concatenate([top_square, cross], axis=1), jnp.concatenate([jnp.transpose(cross), square_in[...]], axis=1)],
        axis=0,
    )
    rotation, _ = solve(gram, lambda r: plan_ref[1, r : r + 1, :], rounds, lambda *_: None)

    pl.delay(1)
    turn = parts_of(rotation)
    for k, (a, b) in enumerate(PEERS + ((0, 0),)):
     if True:
        place = pl.ds(pl.multiple_of(member(a, b) * chunk, chunk), chunk)
        now = product_of(parts_of(jnp.concatenate([tops_now[place], bottoms_in[place]], axis=1)), turn)
        result_out[k, 1] = now[:, BLOCK:]
        send(result_out.at[k, 1], result.at[2 * me + 1], out_send, out_recv, row_of(a, b), after)
        if k < near:
            result_out[k, 0] = now[:, :BLOCK]
            send(result_out.at[k, 0], result.at[2 * me], out_send, out_recv, row_of(a, b), col)
        else:
            result[2 * me] = now[:, :BLOCK]
    pl.delay(1)
    await_bytes(result.at[: 2 * near + 1], out_recv)
    pl.delay(1)
    await_bytes(x_own.at[: 2 * near], in_send)
    await_bytes(tops.at[: 3 * ring * share], sum_send)
    await_bytes(tops.at[: 3 * ring * share], all_send)
    await_bytes(tops, next_send)
    await_bytes(bottoms, next_send)
    await_bytes(turns_out, next_send)
    await_bytes(square_out, next_send)
    await_bytes(shares_c, cross_send)
    await_bytes(half_turned.at[:, : ring * share], all2_send)
    await_bytes(result.at[: 2 * near + 1], out_send)


def body(matrix, plan):
    chunk, pairs, halves, width = matrix.shape
    slots = pairs * halves
    every = chunk * GROUP
    share = BLOCK // ZS
    f32 = jnp.float32
    dma = pltpu.SemaphoreType.DMA
    near, ring = len(PEERS), len(RING)
    vmem = pltpu.VMEM
    result = pl.pallas_call(
        kernel,
        out_shape=jax.ShapeDtypeStruct((slots, chunk, width), f32),
        in_specs=[pl.BlockSpec(memory_space=pltpu.HBM)] * 2,
        out_specs=pl.BlockSpec(memory_space=pltpu.VMEM),
        scratch_shapes=[
            vmem(plan.shape, jnp.int32),
            vmem((slots, chunk, width), f32),
            vmem((every, width), f32),
            vmem((every, width), f32),
            vmem((3, BLOCK, BLOCK), f32),
            vmem((ring, share, BLOCK), f32),
            vmem((ring, 2, share, BLOCK), f32),
            vmem((3, BLOCK, BLOCK), f32),
            vmem((3, share, BLOCK), f32),
            vmem((every, width), f32),
            vmem((every, width), f32),
            vmem((plan.shape[1], 2, WIDTH), f32),
            vmem((plan.shape[1], 2, WIDTH), f32),
            vmem((every, width), f32),
            vmem((BLOCK, BLOCK), f32),
            vmem((BLOCK, BLOCK), f32),
            vmem((every, width), f32),
            vmem((2, BLOCK, WIDTH), f32),
            vmem((2, ring, share, WIDTH), f32),
            vmem((2, BLOCK, BLOCK), f32),
            vmem((2, share, BLOCK), f32),
            vmem((near + 1, 2, chunk, width), f32),
            dma((3,)),
            dma,
            dma((2, 2)),
            dma,
            dma((2,)),
            dma,
            dma((2,)),
            dma,
            dma((7,)),
            dma,
            dma((2,)),
            dma,
            dma,
            dma,
            dma,
        ],
        compiler_params=pltpu.CompilerParams(collective_id=0, has_side_effects=True, vmem_limit_bytes=24 * 2**20),
        cost_estimate=pl.CostEstimate(flops=10**9, bytes_accessed=2 * matrix.size * 4, transcendentals=0),
        name="jacobi_steps",
    )(pltpu.with_memory_space_constraint(matrix.reshape(chunk, slots, width), pltpu.HBM), pltpu.with_memory_space_constraint(plan, pltpu.HBM))
    return result.transpose(1, 0, 2).reshape(matrix.shape)


def solution(mesh):
    in_specs = (P("rows", "cols", None, None), P())
    out_specs = P("rows", "cols", None, None)
    return jax.shard_map(body, mesh=mesh, in_specs=in_specs, out_specs=out_specs, check_vma=False)
```

profile of v0, /device:TPU:1, one launch (start us, length us, event | category | flops | bytes accessed | tf_op | source)
XLA Modules:
  0.0 48.4 jit_solution(10347949042061902471)
XLA Ops:
  0.0 47.2 %jacobi_steps.1 = f32[16,64,128]{2,1,0:T(8,128)S(1)} custom-call(f32[64,16,128]{2,1,0:T(8,128)} %bitcast.5, s32[2,4,256]{2,1,0:T(4,128)} %plan_hbm.1), custom_call_target="tpu_custom_call" | custom-call | flops 1000000000 | bytes 1048576 | tf_op jit(solution)/shard_map/jacobi_steps/pallas_call | solution.py:401
  47.2 1.2 %copy.3 = f32[64,8,2,128]{3,2,1,0:T(2,128)} copy(f32[64,8,2,128]{3,0,2,1:T(8,128)S(1)} %bitcast.4) | data formatting | bytes 1048576 | tf_op jit(solution)/shard_map/reshape | solution.py:449
where the time goes:
time: 48.4 us
  Pallas kernels  47.2 us (98%)
  local copies, waits for them, and re-layouts  1.2 us (2%)
    pallas_call x1, Pallas kernels, body(): pl.pallas_call(kernel, out_shape=jax.ShapeDtypeStruct((slots, chunk, widt...  47.2 us
    reshape x1, local copies, waits for them, and re-layouts, body(): return result.transpose(1, 0, 2).reshape(matrix.shape)  1.2 us

commit v1 on v0

--- a/solution.py
+++ b/solution.py
@@ -46,14 +46,6 @@
     onehot = (rows == partner).astype(jnp.float32).astype(jnp.bfloat16)
     high, middle, low = parts_of(value)
     return product(high, onehot, PLAIN) + (product(middle, onehot, PLAIN) + product(low, onehot, PLAIN))
-
-
-def turned_by(rotation, partner, cosine, sine):
-    if rotation is None:
-        below = lax.broadcasted_iota(jnp.int32, (WIDTH, WIDTH), 0)
-        along = lax.broadcasted_iota(jnp.int32, (WIDTH, WIDTH), 1)
-        return jnp.where(below == along, cosine, 0.0) + jnp.where(below == partner, sine, 0.0)
-    return rotation * cosine + times_onehot(rotation, partner) * sine
 
 
 def columns_moved(value, partner):
@@ -341,15 +333,18 @@
     send(square_out, square_in, next_send, next_recv.at[2 + rounds], rows, after)
 
     pl.delay(1)
-    columns = parts_of(jnp.concatenate([tops[...], bottoms[...]], axis=1))
-    tops_now[...] = product_of(columns, left)
+    below = lax.broadcasted_iota(jnp.int32, (WIDTH, WIDTH), 0)
+    along = lax.broadcasted_iota(jnp.int32, (WIDTH, WIDTH), 1)
     next_rotation = None
     for r in range(rounds):
+        moved = times_onehot(next_rotation, first_plan(r)) if r else None
         await_bytes(turns_in.at[r], next_recv.at[2 + r])
-        next_rotation = turned_by(next_rotation, first_plan(r), turns_in[r, 0:1, :], turns_in[r, 1:2, :])
+        cosine, sine = turns_in[r, 0:1, :], turns_in[r, 1:2, :]
+        if r:
+            next_rotation = next_rotation * cosine + moved * sine
+        else:
+            next_rotation = jnp.where(below == along, cosine, 0.0) + jnp.where(below == first_plan(r), sine, 0.0)
     right = [part[:, BLOCK:] for part in parts_of(next_rotation)]
-    next_columns = parts_of(jnp.concatenate([next_tops[...], next_bottoms[...]], axis=1))
-    bottoms_in[...] = product_of(next_columns, right)
     pl.delay(1)
     await_bytes(square_in, next_recv.at[2 + rounds])
     await_bytes(half_turned.at[:, : ring * share], all2_recv)
@@ -359,21 +354,31 @@
         [jnp.concatenate([top_square, cross], axis=1), jnp.concatenate([jnp.transpose(cross), square_in[...]], axis=1)],
         axis=0,
     )
+    columns = parts_of(jnp.concatenate([tops[...], bottoms[...]], axis=1))
+    tops_now[...] = product_of(columns, left)
+    next_columns = parts_of(jnp.concatenate([next_tops[...], next_bottoms[...]], axis=1))
+    bottoms_in[...] = product_of(next_columns, right)
     rotation, _ = solve(gram, lambda r: plan_ref[1, r : r + 1, :], rounds, lambda *_: None)
 
     pl.delay(1)
     turn = parts_of(rotation)
-    for k, (a, b) in enumerate(PEERS + ((0, 0),)):
-     if True:
-        place = pl.ds(pl.multiple_of(member(a, b) * chunk, chunk), chunk)
-        now = product_of(parts_of(jnp.concatenate([tops_now[place], bottoms_in[place]], axis=1)), turn)
-        result_out[k, 1] = now[:, BLOCK:]
-        send(result_out.at[k, 1], result.at[2 * me + 1], out_send, out_recv, row_of(a, b), after)
-        if k < near:
-            result_out[k, 0] = now[:, :BLOCK]
-            send(result_out.at[k, 0], result.at[2 * me], out_send, out_recv, row_of(a, b), col)
-        else:
-            result[2 * me] = now[:, :BLOCK]
+    targets = PEERS + ((0, 0),)
+    for first, last in ((0, 1), (1, 4), (4, 8)):
+        places = [pl.ds(pl.multiple_of(member(a, b) * chunk, chunk), chunk) for a, b in targets[first:last]]
+        lines = [jnp.concatenate([tops_now[place], bottoms_in[place]], axis=1) for place in places]
+        now = product_of(parts_of(jnp.concatenate(lines, axis=0)), turn)
+        for k in range(first, last):
+            part = now[(k - first) * chunk : (k - first + 1) * chunk]
+            result_out[k, 1] = part[:, BLOCK:]
+            if k < near:
+                result_out[k, 0] = part[:, :BLOCK]
+            else:
+                result[2 * me] = part[:, :BLOCK]
+        for k in range(first, last):
+            row = row_of(*targets[k])
+            send(result_out.at[k, 1], result.at[2 * me + 1], out_send, out_recv, row, after)
+            if k < near:
+                send(result_out.at[k, 0], result.at[2 * me], out_send, out_recv, row, col)
     pl.delay(1)
     await_bytes(result.at[: 2 * near + 1], out_recv)
     pl.delay(1)
@@ -387,6 +392,14 @@
     await_bytes(shares_c, cross_send)
     await_bytes(half_turned.at[:, : ring * share], all2_send)
     await_bytes(result.at[: 2 * near + 1], out_send)
+
+
+def place_kernel(result, out, sem):
+    copies = [pltpu.make_async_copy(result.at[n], out.at[:, n, :], sem) for n in range(result.shape[0])]
+    for copy in copies:
+        copy.start()
+    for copy in copies:
+        copy.wait()
 
 
 def body(matrix, plan):
@@ -446,7 +459,16 @@
         cost_estimate=pl.CostEstimate(flops=10**9, bytes_accessed=2 * matrix.size * 4, transcendentals=0),
         name="jacobi_steps",
     )(pltpu.with_memory_space_constraint(matrix.reshape(chunk, slots, width), pltpu.HBM), pltpu.with_memory_space_constraint(plan, pltpu.HBM))
-    return result.transpose(1, 0, 2).reshape(matrix.shape)
+    placed = pl.pallas_call(
+        place_kernel,
+        out_shape=jax.ShapeDtypeStruct((chunk, slots, width), f32),
+        in_specs=[pl.BlockSpec(memory_space=pltpu.VMEM)],
+        out_specs=pl.BlockSpec(memory_space=pltpu.HBM),
+        scratch_shapes=[dma],
+        compiler_params=pltpu.CompilerParams(vmem_limit_bytes=2**20),
+        name="place",
+    )(result)
+    return placed.reshape(matrix.shape)
 
 
 def solution(mesh):

time: 48.4 us -> 48 us (level)
  local copies, waits for them, and re-layouts: 1.2 us -> 0 us
  Pallas kernels: 47.2 us -> 48 us
    reshape x1 -> x0, local copies, waits for them, and re-layouts: 1.2 us -> none  [body(): return result.transpose(1, 0, 2).reshape(matrix.shape)]
    pallas_call x0 -> x1, Pallas kernels: none -> 0.78 us  [body(): pl.pallas_call(place_kernel, out_shape=jax.ShapeDtypeStruct((chunk, slots...]
where the time goes in v1:
time: 48 us
  Pallas kernels  48 us (100%)
    pallas_call x1, Pallas kernels, body(): pl.pallas_call(kernel, out_shape=jax.ShapeDtypeStruct((slots, chunk, widt...  47.2 us

profile of v1, /device:TPU:1, one launch (start us, length us, event | category | flops | bytes accessed | tf_op | source)
XLA Modules:
  0.0 48.0 jit_solution(7913899968671865547)
XLA Ops:
  0.0 47.2 %jacobi_steps.1.result = f32[16,64,128]{2,1,0:T(8,128)S(1)} custom-call(f32[64,16,128]{2,1,0:T(8,128)} %bitcast.2, s32[2,4,256]{2,1,0:T(4,128)} %plan_hbm.1), custom_call_target="tpu_custom_call" | custom-call | flops 1000000000 | bytes 1048576 | tf_op jit(solution)/shard_map/jacobi_steps/pallas_call | solution.py:414
  47.2 0.8 %place.1 = f32[64,16,128]{2,1,0:T(8,128)} custom-call(f32[16,64,128]{2,1,0:T(8,128)S(1)} %jacobi_steps.1.result), custom_call_target="tpu_custom_call" | custom-call | tf_op jit(solution)/shard_map/place/pallas_call | solution.py:462

commit v2 on v1

--- a/solution.py
+++ b/solution.py
@@ -110,6 +110,8 @@
     shares_b,
     total,
     total_mine,
+    diagonals,
+    diagonal_mine,
     next_tops,
     next_bottoms,
     turns_out,
@@ -277,31 +279,45 @@
     pl.delay(1)
     here = ring_place(0)
     await_bytes(shares_tt, sum_recv.at[0])
-    mine = partial[0, here]
+    own_tt = partial[0, here]
     for n in range(ring):
-        mine = mine + shares_tt[n]
-    total_mine[0] = mine
-    total[0, here] = mine
+        own_tt = own_tt + shares_tt[n]
+    await_bytes(shares_b, sum_recv.at[1])
+    own_b = partial[1:3, here]
+    for n in range(ring):
+        own_b = own_b + shares_b[n]
+    line = lax.broadcasted_iota(jnp.int32, (share, BLOCK), 0) + z * share
+    lane = lax.broadcasted_iota(jnp.int32, (share, BLOCK), 1)
+    mine = jnp.stack([own_b[0], jnp.where(lane >= line, own_tt, own_b[1])], axis=0)
+    total_mine[...] = mine
+    total[:, here] = mine
+    diagonal = jnp.sum(jnp.where(lane == line, own_b[1], 0.0), axis=0, keepdims=True)
+    diagonal_mine[...] = diagonal
+    diagonals[z] = diagonal
     for d in RING:
-        send(total_mine.at[0], total.at[0, here], all_send, all_recv.at[0], ring_row(d), col)
-    await_bytes(shares_b, sum_recv.at[1])
-    mine = partial[1:3, here]
-    for n in range(ring):
-        mine = mine + shares_b[n]
-    total_mine[1:3] = mine
-    total[1:3, here] = mine
-    for d in RING:
-        send(total_mine.at[1:3], total.at[1:3, here], all_send, all_recv.at[1], ring_row(d), col)
+        send(total_mine, total.at[:, here], all_send, all_recv.at[0], ring_row(d), col)
+        send(diagonal_mine, diagonals.at[z], all_send, all_recv.at[1], ring_row(d), col)
     pl.delay(1)
     cross_products(1)
     pl.delay(1)
-    await_bytes(total.at[0, : ring * share], all_recv.at[0])
-    await_bytes(total.at[1:3, : ring * share], all_recv.at[1])
-
-    pl.delay(1)
-    cross = total[1]
+    await_bytes(total.at[:, : ring * share], all_recv.at[0])
+    await_bytes(diagonals.at[:ring], all_recv.at[1])
+
+    pl.delay(1)
+    cross = total[0]
+    packed = total[1]
+    flipped = jnp.transpose(packed)
+    line = lax.broadcasted_iota(jnp.int32, (BLOCK, BLOCK), 0)
+    lane = lax.broadcasted_iota(jnp.int32, (BLOCK, BLOCK), 1)
+    diagonal = jnp.sum(diagonals[...], axis=0)
+    top_gram = jnp.where(lane >= line, packed, flipped)
+    bottom_gram = jnp.where(lane == line, diagonal, jnp.where(lane < line, packed, flipped))
     gram = jnp.concatenate(
-        [jnp.concatenate([total[0], jnp.transpose(cross)], axis=1), jnp.concatenate([cross, total[2]], axis=1)], axis=0
+        [
+            jnp.concatenate([top_gram, jnp.transpose(cross)], axis=1),
+            jnp.concatenate([cross, bottom_gram], axis=1),
+        ],
+        axis=0,
     )
     rounds = plan_ref.shape[1]
 
@@ -384,7 +400,8 @@
     pl.delay(1)
     await_bytes(x_own.at[: 2 * near], in_send)
     await_bytes(tops.at[: 3 * ring * share], sum_send)
-    await_bytes(tops.at[: 3 * ring * share], all_send)
+    await_bytes(tops.at[: 2 * ring * share], all_send)
+    await_bytes(diagonals.at[:ring], all_send)
     await_bytes(tops, next_send)
     await_bytes(bottoms, next_send)
     await_bytes(turns_out, next_send)
@@ -424,8 +441,10 @@
             vmem((3, BLOCK, BLOCK), f32),
             vmem((ring, share, BLOCK), f32),
             vmem((ring, 2, share, BLOCK), f32),
-            vmem((3, BLOCK, BLOCK), f32),
-            vmem((3, share, BLOCK), f32),
+            vmem((2, BLOCK, BLOCK), f32),
+            vmem((2, share, BLOCK), f32),
+            vmem((ZS, 1, BLOCK), f32),
+            vmem((1, BLOCK), f32),
             vmem((every, width), f32),
             vmem((every, width), f32),
             vmem((plan.shape[1], 2, WIDTH), f32),

time: 48 us -> 47.2 us (0.983)
  Pallas kernels: 48 us -> 47.1 us
    pallas_call x1, Pallas kernels: 47.2 us -> 46.3 us  [body(): pl.pallas_call(kernel, out_shape=jax.ShapeDtypeStruct((slots, chunk, widt...]
where the time goes in v2:
time: 47.2 us; the launch traced here: 47.1 us
  Pallas kernels  47.1 us (100%)
    pallas_call x1, Pallas kernels, body(): pl.pallas_call(kernel, out_shape=jax.ShapeDtypeStruct((slots, chunk, widt...  46.3 us

profile of v2, /device:TPU:1, one launch (start us, length us, event | category | flops | bytes accessed | tf_op | source)
XLA Modules:
  0.0 47.1 jit_solution(12985888841696596094)
XLA Ops:
  0.0 46.3 %jacobi_steps.1.result = f32[16,64,128]{2,1,0:T(8,128)S(1)} custom-call(f32[64,16,128]{2,1,0:T(8,128)} %bitcast.2, s32[2,4,256]{2,1,0:T(4,128)} %plan_hbm.1), custom_call_target="tpu_custom_call" | custom-call | flops 1000000000 | bytes 1048576 | tf_op jit(solution)/shard_map/jacobi_steps/pallas_call | solution.py:431
  46.3 0.8 %place.1 = f32[64,16,128]{2,1,0:T(8,128)} custom-call(f32[16,64,128]{2,1,0:T(8,128)S(1)} %jacobi_steps.1.result), custom_call_target="tpu_custom_call" | custom-call | tf_op jit(solution)/shard_map/place/pallas_call | solution.py:481

commit v3 on v2

--- a/solution.py
+++ b/solution.py
@@ -252,18 +252,18 @@
     both_early = full_product(bottoms_early, jnp.concatenate([tops_early, bottoms_early], axis=1), FIRST)
     arrived(bottoms, 1, 1)
     pl.delay(1)
+    @pl.when(col % 2 == 1)
+    def _():
+        send(tops, next_tops, next_send, next_recv.at[0], rows, after)
+
+    send(bottoms, next_bottoms, next_send, next_recv.at[1], rows, after)
+    pl.delay(1)
     bottoms_late = lines_of(bottoms, 1)
     both = both_early + full_product(bottoms_late, jnp.concatenate([tops_late, bottoms_late], axis=1), FIRST)
     partial[1] = both[:, :BLOCK]
     partial[2] = both[:, BLOCK:]
     for n, d in enumerate(RING):
         send(partial.at[1:3, ring_place(d)], shares_b.at[n], sum_send, sum_recv.at[1], ring_row(d), col)
-
-    @pl.when(col % 2 == 1)
-    def _():
-        send(tops, next_tops, next_send, next_recv.at[0], rows, after)
-
-    send(bottoms, next_bottoms, next_send, next_recv.at[1], rows, after)
 
     def cross_products(half):
         arrived_block = (next_tops, next_bottoms)[half]
@@ -351,6 +351,8 @@
     pl.delay(1)
     below = lax.broadcasted_iota(jnp.int32, (WIDTH, WIDTH), 0)
     along = lax.broadcasted_iota(jnp.int32, (WIDTH, WIDTH), 1)
+    columns = parts_of(jnp.concatenate([tops[...], bottoms[...]], axis=1))
+    tops_now[...] = product_of(columns, left)
     next_rotation = None
     for r in range(rounds):
         moved = times_onehot(next_rotation, first_plan(r)) if r else None
@@ -370,8 +372,6 @@
         [jnp.concatenate([top_square, cross], axis=1), jnp.concatenate([jnp.transpose(cross), square_in[...]], axis=1)],
         axis=0,
     )
-    columns = parts_of(jnp.concatenate([tops[...], bottoms[...]], axis=1))
-    tops_now[...] = product_of(columns, left)
     next_columns = parts_of(jnp.concatenate([next_tops[...], next_bottoms[...]], axis=1))
     bottoms_in[...] = product_of(next_columns, right)
     rotation, _ = solve(gram, lambda r: plan_ref[1, r : r + 1, :], rounds, lambda *_: None)

time: 47.2 us -> 46.6 us (0.987)
  Pallas kernels: 47.1 us -> 46.5 us
    pallas_call x1, Pallas kernels: 46.3 us -> 45.7 us  [body(): pl.pallas_call(kernel, out_shape=jax.ShapeDtypeStruct((slots, chunk, widt...]
where the time goes in v3:
time: 46.6 us; the launch traced here: 46.5 us
  Pallas kernels  46.5 us (100%)
    pallas_call x1, Pallas kernels, body(): pl.pallas_call(kernel, out_shape=jax.ShapeDtypeStruct((slots, chunk, widt...  45.7 us

profile of v3, /device:TPU:1, one launch (start us, length us, event | category | flops | bytes accessed | tf_op | source)
XLA Modules:
  0.0 46.5 jit_solution(2641810026176596359)
XLA Ops:
  0.0 45.7 %jacobi_steps.1.result = f32[16,64,128]{2,1,0:T(8,128)S(1)} custom-call(f32[64,16,128]{2,1,0:T(8,128)} %bitcast.2, s32[2,4,256]{2,1,0:T(4,128)} %plan_hbm.1), custom_call_target="tpu_custom_call" | custom-call | flops 1000000000 | bytes 1048576 | tf_op jit(solution)/shard_map/jacobi_steps/pallas_call | solution.py:431
  45.7 0.8 %place.1 = f32[64,16,128]{2,1,0:T(8,128)} custom-call(f32[16,64,128]{2,1,0:T(8,128)S(1)} %jacobi_steps.1.result), custom_call_target="tpu_custom_call" | custom-call | tf_op jit(solution)/shard_map/place/pallas_call | solution.py:481

commit v4 on v3

--- a/solution.py
+++ b/solution.py
@@ -326,9 +326,9 @@
 
     def tell(r, cosine, sine):
         turns_out[r] = jnp.concatenate([cosine, sine], axis=0)
-        send(turns_out.at[r], turns_in.at[r], next_send, next_recv.at[2 + r], rows, after)
 
     rotation, image = solve(gram, first_plan, rounds, tell)
+    send(turns_out, turns_in, next_send, next_recv.at[2], rows, after)
     pl.delay(1)
     await_bytes(shares_c.at[0], cross_recv.at[0])
     await_bytes(shares_c.at[1], cross_recv.at[1])
@@ -356,7 +356,8 @@
     next_rotation = None
     for r in range(rounds):
         moved = times_onehot(next_rotation, first_plan(r)) if r else None
-        await_bytes(turns_in.at[r], next_recv.at[2 + r])
+        if r == 0:
+            await_bytes(turns_in, next_recv.at[2])
         cosine, sine = turns_in[r, 0:1, :], turns_in[r, 1:2, :]
         if r:
             next_rotation = next_rotation * cosine + moved * sine

time: 46.6 us -> 46.6 us (level)
  no operation moved by 1% of the time
where the time goes in v4:
time: 46.6 us; the launch traced here: 46.5 us
  Pallas kernels  46.5 us (100%)
    pallas_call x1, Pallas kernels, body(): pl.pallas_call(kernel, out_shape=jax.ShapeDtypeStruct((slots, chunk, widt...  45.7 us

profile of v4, /device:TPU:1, one launch (start us, length us, event | category | flops | bytes accessed | tf_op | source)
XLA Modules:
  0.0 46.5 jit_solution(14289263532464489550)
XLA Ops:
  0.0 45.7 %jacobi_steps.1.result = f32[16,64,128]{2,1,0:T(8,128)S(1)} custom-call(f32[64,16,128]{2,1,0:T(8,128)} %bitcast.2, s32[2,4,256]{2,1,0:T(4,128)} %plan_hbm.1), custom_call_target="tpu_custom_call" | custom-call | flops 1000000000 | bytes 1048576 | tf_op jit(solution)/shard_map/jacobi_steps/pallas_call | solution.py:432
  45.7 0.8 %place.1 = f32[64,16,128]{2,1,0:T(8,128)} custom-call(f32[16,64,128]{2,1,0:T(8,128)S(1)} %jacobi_steps.1.result), custom_call_target="tpu_custom_call" | custom-call | tf_op jit(solution)/shard_map/place/pallas_call | solution.py:482
